TPU v7x, 32 devices: a whole 2x2x4 slice. The times are simulated.
32 devices in a mesh: rows: 8 (over z, x), cols: 4 (over y, core).
Axes of the slice: x: 2, y: 2, z: 4, core: 2. Of those that a mesh axis runs over, the one named last changes fastest.
Arguments:
- grad_out: bfloat16 [32, 512, 192], P(('rows', 'cols')), may hold values from -6 to 6
- inputs: bfloat16 [64, 1024, 192], P('rows', 'cols'), may hold values from -6 to 6
- weight: bfloat16 [3, 3, 192, 192], replicated, may hold values from -0.15625 to 0.15625
Outputs:
- input_grad: bfloat16 [64, 1024, 192], P('rows', 'cols')
- filter_grad: float32 [3, 3, 192, 192], replicated
All inputs are finite; a program needn't handle non-finite values.
Results may differ from a plain program's by a relative error of at most 0.0028.
Values may be sent and summed in bfloat16 or wider, within the bound.
A program may use at most 64 MiB of HBM per device.

v0:
```python
import math

import jax
import jax.numpy as jnp
from jax import lax
from jax.sharding import PartitionSpec as P


def shifted(x, axis, by):
    devices = lax.axis_size(axis)
    pairs = [(i, i + by) for i in range(devices) if 0 <= i + by < devices]
    return lax.ppermute(x, axis, pairs)


def tap_products(out_block, flat_weight):
    chans = flat_weight.shape[0]
    flat = out_block.reshape(-1, chans)
    products = jnp.dot(flat, flat_weight, preferred_element_type=jnp.float32)
    return products.reshape(out_block.shape[0], out_block.shape[1], 3, 3, chans)


def assemble(products, count_rows, count_cols):
    rows_even = products[:count_rows, :, 1]
    rows_odd = products[:count_rows, :, 2] + products[1 : count_rows + 1, :, 0]

    def columns(mixed):
        even = mixed[:, :count_cols, 1]
        odd = mixed[:, :count_cols, 2] + mixed[:, 1 : count_cols + 1, 0]
        return jnp.stack([even, odd], axis=2)

    placed = jnp.stack([columns(rows_even), columns(rows_odd)], axis=1)
    return placed.reshape(2 * count_rows, 2 * count_cols, products.shape[-1])


def filter_terms(input_band, out_band, row_taps):
    count_rows, count_cols, chans = out_band.shape
    split = input_band.reshape(count_rows + 1, 2, count_cols + 1, 2, chans)
    offsets = ((0, 0), (0, 1), (1, 0))
    pieces = []
    for row_tap in row_taps:
        start_row, parity_row = offsets[row_tap]
        for col_tap in range(3):
            start_col, parity_col = offsets[col_tap]
            pieces.append(
                split[
                    start_row : start_row + count_rows,
                    parity_row,
                    start_col : start_col + count_cols,
                    parity_col,
                ]
            )
    stacked = jnp.stack(pieces, axis=2).reshape(count_rows * count_cols, len(pieces) * chans)
    flat_out = out_band.reshape(count_rows * count_cols, chans)
    return lax.dot_general(
        stacked, flat_out, (((0,), (0,)), ((), ())), preferred_element_type=jnp.float32
    )


def per_device(grad_out, inputs, weight):
    chans = weight.shape[2]
    rows_local, cols_local = (inputs.shape[0], inputs.shape[1])
    half_rows, half_cols = (rows_local // 2, cols_local // 2)
    whole = lax.all_gather(grad_out, "cols", axis=0, tiled=True)
    out_grad = lax.dynamic_slice_in_dim(whole, lax.axis_index("cols") * half_cols, half_cols, 1)
    flat_weight = jnp.transpose(weight, (3, 0, 1, 2)).reshape(chans, 9 * chans)
    above = shifted(inputs[-1:], "rows", 1)
    with_above = jnp.concatenate([above, inputs], axis=0)
    left = shifted(with_above[:, -1:], "cols", 1)
    input_band = jnp.pad(jnp.concatenate([left, with_above], axis=1), ((0, 1), (0, 1), (0, 0)))
    positions = half_rows * lax.axis_size("rows") * (half_cols * lax.axis_size("cols"))
    scale = 1.0 / math.sqrt(positions)
    buckets = []
    for row_tap in range(3):
        terms = filter_terms(input_band, out_grad, (row_tap,))
        buckets.append(lax.psum(terms, ("rows", "cols")))
    summed = jnp.concatenate(buckets, axis=0)
    filter_grad = summed.reshape(3, 3, chans, chans) * scale
    framed = jnp.pad(out_grad, ((1, 1), (1, 1), (0, 0)))
    placed = assemble(tap_products(framed, flat_weight), half_rows + 1, half_cols + 1)
    extended = placed[1:, 1:]
    below = shifted(extended[:1].astype(jnp.bfloat16), "rows", -1).astype(jnp.float32)
    own_rows = extended[1:].at[-1].add(below[0])
    right = shifted(own_rows[:, :1], "cols", -1)
    input_grad = own_rows[:, 1:].at[:, -1].add(right[:, 0])
    return (input_grad.astype(jnp.bfloat16), filter_grad)


def solution(mesh):
    in_specs = (P(("rows", "cols"), None, None), P("rows", "cols", None), P())
    out_specs = (P("rows", "cols", None), P())
    return jax.shard_map(
        per_device, mesh=mesh, in_specs=in_specs, out_specs=out_specs, check_vma=False
    )
```

profile of v0, /device:TPU:1, one launch (start us, length us, event | category | flops | bytes accessed | tf_op | source)
XLA Modules:
  0.0 207.7 jit_solution(10896684272660905231)
XLA Ops:
  8.2 3.9 %collective-permute-start.2 = (bf16[1,256,192]{1,2,0:T(8,128)(2,1)S(1)}, bf16[1,256,192]{1,2,0:T(8,128)(2,1)S(1)}, u32[]{:S(2)}, u32[]{:S(2)}) collective-permute-start(bf16[1,256,192]{1,2,0:T(8,128)(2,1)S(1)} %slice.137), channel_id=1, source_target_pairs={{0,4},{4,8},{8,12},{12,16},{16,20},{20,24},{24,28},{1,5},{5,9},{9,... | collective-permute-start | bytes 294920 | tf_op jit(solution)/shard_map/ppermute | solution.py:12
  12.1 9.6 %all_gather.3 = bf16[4,512,192]{1,2,0:T(8,128)(2,1)S(1)} all-gather(bf16[1,512,192]{1,2,0:T(8,128)(2,1)} %param.7), channel_id=1, replica_groups=mesh['rows'=8,'cols'=4] {'cols'}, dimensions={0}, use_global_device_ids=true | all-gather | bytes 983040 | tf_op jit(solution)/shard_map/all_gather | solution.py:63
  22.0 1.2 fusion.1
  24.0 1.2 maximum_bitcast_fusion.1
  25.5 2.7 %collective-permute-start.3 = (bf16[9,1,192]{1,2,0:T(8,128)(2,1)S(1)}, bf16[9,1,192]{1,2,0:T(8,128)(2,1)S(1)}, u32[]{:S(2)}, u32[]{:S(2)}) collective-permute-start(bf16[9,1,192]{1,2,0:T(8,128)(2,1)S(1)} %slice.163), channel_id=1, source_target_pairs={{0,1},{1,2},{2,3},{4,5},{5,6},{6,7},{8,9},{9,10},{10,11},{12,13},{... | collective-permute-start | bytes 10376 | tf_op jit(solution)/shard_map/ppermute | solution.py:12
  28.2 1.3 maximum_bitcast_fusion
  29.5 3.8 %collective-permute-done.3 = bf16[9,1,192]{1,2,0:T(8,128)(2,1)S(1)} collective-permute-done((bf16[9,1,192]{1,2,0:T(8,128)(2,1)S(1)}, bf16[9,1,192]{1,2,0:T(8,128)(2,1)S(1)}, u32[]{:S(2)}, u32[]{:S(2)}) %collective-permute-start.3) | collective-permute-done | bytes 3488 | tf_op jit(solution)/shard_map/ppermute | solution.py:12
  33.9 1.7 copy.92
  35.6 2.6 %pad.13.clone = bf16[10,258,192]{2,1,0:T(8,128)(2,1)} pad(bf16[9,257,192]{2,1,0:T(8,128)(2,1)} %copy.92, bf16[]{:T(256)} %constant.66.clone.1), padding=0_1x0_1x0_0 | pad | bytes 1878914 | tf_op jit(solution)/shard_map/jit(_pad)/pad | solution.py:69
  38.2 3.1 %reshape.97 = bf16[5,2,129,2,192]{4,3,2,1,0:T(2,128)(2,1)S(1)} reshape(bf16[10,258,192]{2,1,0:T(8,128)(2,1)} %pad.13.clone) | data formatting | bytes 1981440 | tf_op jit(solution)/shard_map/reshape | solution.py:37
  41.3 4.5 %fusion.18 = (bf16[4,1,128,1,192]{4,3,2,1,0:T(2,128)(2,1)S(1)}, bf16[4,1,128,1,192]{4,3,2,1,0:T(2,128)(2,1)}, bf16[4,1,128,1,192]{4,3,2,1,0:T(2,128)(2,1)S(1)}, ...) fusion(bf16[5,2,129,2,192]{4,3,2,1,0:T(2,128)(2,1)S(1)} %reshape.97), kind=kLoop, calls=%fused_computation.36 | loop fusion | bytes 3538944 | tf_op jit(solution)/shard_map/slice | solution.py:45
  45.8 1.2 copy.77
  47.0 1.2 copy.76
  48.3 1.3 copy.75
  50.1 1.2 copy.81
  51.4 1.9 copy.80
  55.8 1.2 fusion.9
  56.9 1.2 fusion.6
  59.7 1.2 fusion.3
  60.9 1.5 pad_maximum_fusion
  62.5 1.4 copy.73
  63.8 2.9 %reshape.96 = f32[10,258,192]{2,1,0:T(8,128)} reshape(f32[5,2,129,2,192]{4,3,2,1,0:T(2,128)S(1)} %copy.73) | data formatting | bytes 3962880 | tf_op jit(solution)/shard_map/reshape | solution.py:32
  67.7 1.3 collective-permute-start
  69.0 1.8 slice.157
  70.8 3.6 %collective-permute-done = bf16[1,257,192]{2,1,0:T(8,128)(2,1)S(1)} collective-permute-done((bf16[1,257,192]{2,1,0:T(8,128)(2,1)S(1)}, bf16[1,257,192]{2,1,0:T(8,128)(2,1)S(1)}, u32[]{:S(2)}, u32[]{:S(2)}) %collective-permute-start) | collective-permute-done | bytes 98720 | tf_op jit(solution)/shard_map/ppermute | solution.py:12
  75.4 1.9 collective-permute-start.1
  77.6 4.8 %collective-permute-done.1 = f32[8,1,192]{2,1,0:T(1,128)S(1)} collective-permute-done((f32[8,1,192]{2,1,0:T(1,128)S(1)}, f32[8,1,192]{2,1,0:T(1,128)S(1)}, u32[]{:S(2)}, u32[]{:S(2)}) %collective-permute-start.1) | collective-permute-done | bytes 6176 | tf_op jit(solution)/shard_map/ppermute | solution.py:12
  82.4 1.3 copy.88
  83.7 111.2 %all-reduce.5.cloned.1.call-done = (f32[576,192]{0,1:T(8,128)}, f32[576,192]{0,1:T(8,128)}, f32[576,192]{0,1:T(8,128)}) async-done(((f32[576,192]{0,1:T(8,128)}, f32[576,192]{0,1:T(8,128)}, f32[576,192]{0,1:T(8,128)}), (f32[576,192]{0,1:T(8,128)}, f32[576,192]{0,1:T(8,128)}, f32[576,192]{0,1:T(8,128)})) %all-reduce.5.cloned.1.call-update) | async-done | bytes 1327120 | tf_op jit(solution)/shard_map/psum | solution.py:75
  194.9 1.6 concatenate.15
  196.5 1.2 broadcast_multiply_fusion
  197.7 3.1 %copy.87 = f32[1728,192]{1,0:T(8,128)} copy(f32[1728,192]{0,1:T(8,128)} %broadcast_multiply_fusion) | data formatting | bytes 2654208 | tf_op jit(solution)/shard_map/mul | solution.py:77
  (38 shorter events, 9.9 us)
Async XLA Ops:
  7.2 14.8 %copy-start = (bf16[3,3,192,192]{3,2,1,0:T(8,128)(2,1)S(1)}, bf16[3,3,192,192]{3,2,1,0:T(8,128)(2,1)}, u32[]{:S(2)}) copy-start(bf16[3,3,192,192]{3,2,1,0:T(8,128)(2,1)} %param.9) | copy-start | bytes 1990660
  7.2 187.7 %all-reduce.5.cloned.1.call-start = ((), (), s32[]{:S(2)}) async-start(), calls=%async_computation | async-start | bytes 2949120 | tf_op jit(solution)/shard_map/psum | solution.py:75
  8.2 17.0 %collective-permute-start.2 = (bf16[1,256,192]{1,2,0:T(8,128)(2,1)S(1)}, bf16[1,256,192]{1,2,0:T(8,128)(2,1)S(1)}, u32[]{:S(2)}, u32[]{:S(2)}) collective-permute-start(bf16[1,256,192]{1,2,0:T(8,128)(2,1)S(1)} %slice.137), channel_id=1, source_target_pairs={{0,4},{4,8},{8,12},{12,16},{16,20},{20,24},{24,28},{1,5},{5,9},{9,... | collective-permute-start | bytes 294920 | tf_op jit(solution)/shard_map/ppermute | solution.py:12
  24.0 1.3 copy-start.4
  25.5 7.7 %collective-permute-start.3 = (bf16[9,1,192]{1,2,0:T(8,128)(2,1)S(1)}, bf16[9,1,192]{1,2,0:T(8,128)(2,1)S(1)}, u32[]{:S(2)}, u32[]{:S(2)}) collective-permute-start(bf16[9,1,192]{1,2,0:T(8,128)(2,1)S(1)} %slice.163), channel_id=1, source_target_pairs={{0,1},{1,2},{2,3},{4,5},{5,6},{6,7},{8,9},{9,10},{10,11},{12,13},{... | collective-permute-start | bytes 10376 | tf_op jit(solution)/shard_map/ppermute | solution.py:12
  48.3 5.0 %copy-start.3 = (bf16[4,1,128,1,192]{4,3,2,1,0:T(2,128)(2,1)S(1)}, bf16[4,1,128,1,192]{4,3,2,1,0:T(2,128)(2,1)}, u32[]{:S(2)}) copy-start(bf16[4,1,128,1,192]{4,3,2,1,0:T(2,128)(2,1)} %get-tuple-element.50) | copy-start | bytes 589828
  55.3 2.8 %copy-start.2 = (bf16[4,1,128,1,192]{4,3,2,1,0:T(2,128)(2,1)S(1)}, bf16[4,1,128,1,192]{4,3,2,1,0:T(2,128)(2,1)}, u32[]{:S(2)}) copy-start(bf16[4,1,128,1,192]{4,3,2,1,0:T(2,128)(2,1)} %get-tuple-element.46) | copy-start | bytes 589828
  59.2 1.7 copy-start.1
  67.7 6.7 %collective-permute-start = (bf16[1,257,192]{2,1,0:T(8,128)(2,1)S(1)}, bf16[1,257,192]{2,1,0:T(8,128)(2,1)S(1)}, u32[]{:S(2)}, u32[]{:S(2)}) collective-permute-start(bf16[1,257,192]{2,1,0:T(8,128)(2,1)S(1)} %slice.187), channel_id=1, source_target_pairs={{4,0},{8,4},{12,8},{16,12},{20,16},{24,20},{28,24},{5,1},{9,5},{13... | collective-permute-start | bytes 296072 | tf_op jit(solution)/shard_map/ppermute | solution.py:12
  75.4 6.9 %collective-permute-start.1 = (f32[8,1,192]{2,1,0:T(1,128)S(1)}, f32[8,1,192]{2,1,0:T(1,128)S(1)}, u32[]{:S(2)}, u32[]{:S(2)}) collective-permute-start(f32[8,1,192]{2,1,0:T(1,128)S(1)} %slice.162), channel_id=1, source_target_pairs={{1,0},{2,1},{3,2},{5,4},{6,5},{7,6},{9,8},{10,9},{11,10},{13,12},{... | collective-permute-start | bytes 18440 | tf_op jit(solution)/shard_map/ppermute | solution.py:12
Sparse Core Ops, SparseCore 0:
  61.0 133.8 all-reduce.4
where the time goes:
time: 209 us; the launch traced here: 208 us
  waiting for transfers between devices  123 us (59%)
  local copies, waits for them, and re-layouts  36.9 us (18%)
  between operations  14.3 us (7%)
  starting transfers between devices  9.84 us (5%)
  blocking collectives  9.63 us (5%)
  other arithmetic  8.95 us (4%)
  matrix products  4.68 us (2%)
    psum x1, waiting for transfers between devices, per_device(): buckets.append(lax.psum(terms, ('rows', 'cols')))  111 us
    slice x10, local copies, waits for them, and re-layouts, filter_terms(): split[start_row:start_row + count_rows, parity_row, start_col:start_col +...  13.3 us
    ppermute x4, waiting for transfers between devices, shifted(): return lax.ppermute(x, axis, pairs)  12.1 us
    ppermute x4, starting transfers between devices, shifted(): return lax.ppermute(x, axis, pairs)  9.8 us
    all_gather x1, blocking collectives, per_device(): whole = lax.all_gather(grad_out, 'cols', axis=0, tiled=True)  9.63 us
  transfers between devices with their start and end apart: 5, of which 4 were waited for; matrix products, arithmetic and copies ran while one was open for 8% of the time, Pallas kernels for 0%

commit v1 on v0

v1 whole, which is shorter than its diff:
```python
import functools
import math

import jax
import jax.numpy as jnp
from jax import lax
from jax.experimental import pallas as pl
from jax.experimental.pallas import tpu as pltpu
from jax.sharding import PartitionSpec as P

MESH = pl.DeviceIdType.MESH
LANES = 128
EDGE = 16
F32 = jnp.float32
BF16 = jnp.bfloat16
PARITY = (1, 0, 1)
SHIFT = (1, 0, 0)


def spread_matrix(size, transpose):
    half = size // 2
    i = lax.broadcasted_iota(jnp.int32, (size, size), 1 if transpose else 0)
    k = lax.broadcasted_iota(jnp.int32, (size, size), 0 if transpose else 1)
    source = jnp.where(i < half, 2 * i, 2 * (i - half) + 1)
    return jnp.where(k == source, 1.0, 0.0).astype(BF16)


def nt(a, b):
    return lax.dot_general(a, b, (((1,), (1,)), ((), ())), preferred_element_type=F32)


def step_kernel(
    n_rows, n_cols, scale,
    g_ref, x_hbm, w_hbm, ig_ref, sum_ref,
    x, w, gm, gh, gs, xt, part, pair, outbox, inbox, full,
    load_sem, main_s, main_r, halo_s, halo_r, up_s, pair_s, pair_r,
    rs_s, rs_r, ag_s, ag_r, fw_s, fw_r,
):
    r = lax.axis_index("rows")
    c = lax.axis_index("cols")
    core = lax.rem(c, 2)
    depth = n_cols // 2
    chips = n_rows * depth
    chip = r * depth + c // 2
    partner = (r, c + 1 - 2 * core)
    half_rows = n_cols
    half_cols = g_ref.shape[1] // n_cols
    chans = g_ref.shape[2]
    count = outbox.shape[0]
    base = core * count
    devices = n_rows * n_cols
    me = r * n_cols + c

    barrier = pltpu.get_barrier_semaphore()

    def greet(i, _):
        other = lax.rem(me + i, devices)
        pl.semaphore_signal(
            barrier, inc=1, device_id=(other // n_cols, lax.rem(other, n_cols)), device_id_type=MESH
        )
        return 0

    lax.fori_loop(1, devices, greet, 0)
    load_x = pltpu.make_async_copy(x_hbm, x, load_sem.at[0])
    load_w = pltpu.make_async_copy(w_hbm, w, load_sem.at[1])
    load_x.start()
    load_w.start()

    @pl.when(c == n_cols - 1)
    def _():
        gh[...] = jnp.zeros_like(gh)

    @pl.when(r == n_rows - 1)
    def _():
        gm[half_rows] = jnp.zeros(gm.shape[1:], BF16)
        gh[half_rows] = jnp.zeros(gh.shape[1:], BF16)

    for q in range(n_cols):

        @pl.when(c == q)
        def _():
            gm[q] = g_ref[0, q * half_cols : (q + 1) * half_cols]
            if q < n_cols - 1:
                gh[q] = g_ref[0, (q + 1) * half_cols : (q + 1) * half_cols + EDGE]

    pl.semaphore_wait(barrier, devices - 1)

    def main_copy(q, row, slot, send):
        return pltpu.make_async_remote_copy(
            src_ref=g_ref.at[0, pl.ds(q * half_cols, half_cols)], dst_ref=gm.at[slot],
            send_sem=send, recv_sem=main_r.at[slot], device_id=(row, q), device_id_type=MESH,
        )

    def halo_copy(q, row, slot, send):
        return pltpu.make_async_remote_copy(
            src_ref=g_ref.at[0, pl.ds((q + 1) * half_cols, EDGE)], dst_ref=gh.at[slot],
            send_sem=send, recv_sem=halo_r.at[slot], device_id=(row, q), device_id_type=MESH,
        )

    def outgoing(act):
        for q in range(n_cols):

            @pl.when(c != q)
            def _():
                act(main_copy(q, r, c, main_s.at[q]))
                if q < n_cols - 1:
                    act(halo_copy(q, r, c, halo_s.at[q]))

            @pl.when((c == 0) & (r > 0))
            def _():
                act(main_copy(q, r - 1, half_rows, up_s.at[0, q]))
                if q < n_cols - 1:
                    act(halo_copy(q, r - 1, half_rows, up_s.at[1, q]))

    outgoing(lambda copy: copy.start())

    load_x.wait()
    width = x.shape[1]
    sort = spread_matrix(width, False)
    eye = (
        lax.broadcasted_iota(jnp.int32, (chans, chans), 0)
        == lax.broadcasted_iota(jnp.int32, (chans, chans), 1)
    )
    eye = jnp.where(eye, 1.0, 0.0).astype(BF16)
    for p in range(x.shape[0]):
        ordered = jnp.dot(sort, x[p], preferred_element_type=F32).astype(BF16)
        turned = nt(eye, ordered).astype(BF16)
        i = p // 2
        for s in range(2):
            xt[p % 2, s, :, i * half_cols : (i + 1) * half_cols] = turned[
                :, s * half_cols : (s + 1) * half_cols
            ]

    for i in range(half_rows + 1):
        if i < half_rows:
            arrives = c != i
        else:
            arrives = r < n_rows - 1

        @pl.when(arrives)
        def _():
            main_copy(0, r, i, main_s.at[0]).wait_recv()

        @pl.when(arrives & (c < n_cols - 1))
        def _():
            halo_copy(0, r, i, halo_s.at[0]).wait_recv()

        row = jnp.concatenate([gm[i], gh[i]], axis=0).astype(F32)
        gs[i] = row[1 : half_cols + 1].astype(BF16)

    def grad(down, along):
        src = gs if along else gm
        return src[down : down + half_rows].reshape(half_rows * half_cols, chans)

    split = chans // 2
    part[2 * count - 1] = jnp.zeros(part.shape[1:], F32)
    for a in range(3):
        for b in range(3):
            t = 3 * a + b
            terms = jnp.dot(
                xt[PARITY[a], PARITY[b]], grad(SHIFT[a], SHIFT[b]), preferred_element_type=F32
            )
            part[3 * t] = terms[:split, :LANES]
            part[3 * t + 1] = terms[split:, :LANES]
            part[3 * t + 2] = jnp.concatenate([terms[:split, LANES:], terms[split:, LANES:]], axis=1)

    def pair_copy(j):
        return pltpu.make_async_remote_copy(
            src_ref=part.at[(1 - core) * count + j], dst_ref=pair.at[j],
            send_sem=pair_s.at[j], recv_sem=pair_r.at[j], device_id=partner, device_id_type=MESH,
        )

    for j in range(count):
        pair_copy(j).start()

    owners = [(j * chips) // count for j in range(count)]

    def scatter_copy(j):
        return pltpu.make_async_remote_copy(
            src_ref=outbox.at[j], dst_ref=inbox.at[chip],
            send_sem=rs_s.at[j], recv_sem=rs_r.at[chip],
            device_id=(owners[j] // depth, 2 * (owners[j] % depth) + core), device_id_type=MESH,
        )

    for j in range(count):
        pair_copy(j).wait_recv()
        outbox[j] = (part[base + j] + pair[j]).astype(BF16)

        @pl.when(chip != owners[j])
        def _():
            scatter_copy(j).start()

    load_w.wait()
    back = spread_matrix(width, True)

    def tap(a, b):
        return nt(grad(SHIFT[a], SHIFT[b]), w[a, b])

    for odd in range(2):
        taps = (0, 2) if odd else (1,)
        even_cols = sum(tap(a, 1) for a in taps).astype(BF16)
        odd_cols = sum(tap(a, 0) + tap(a, 2) for a in taps).astype(BF16)
        for i in range(half_rows):
            cut = slice(i * half_cols, (i + 1) * half_cols)
            both = jnp.concatenate([even_cols[cut], odd_cols[cut]], axis=0)
            ig_ref[2 * i + odd] = jnp.dot(back, both, preferred_element_type=F32).astype(BF16)

    mine = (chip * count + chips - 1) // chips
    owns = (mine < count) & ((mine * chips) // count == chip)

    def gather_copy(other):
        return pltpu.make_async_remote_copy(
            src_ref=full.at[base + mine], dst_ref=full.at[base + mine],
            send_sem=ag_s.at[other], recv_sem=ag_r.at[mine],
            device_id=(other // depth, 2 * lax.rem(other, depth) + core), device_id_type=MESH,
        )

    @pl.when(owns)
    def _():
        def collect(i, total):
            source = lax.rem(chip + i, chips)
            pltpu.make_async_remote_copy(
                src_ref=outbox.at[0], dst_ref=inbox.at[source],
                send_sem=rs_s.at[0], recv_sem=rs_r.at[source], device_id=partner, device_id_type=MESH,
            ).wait_recv()
            return total + inbox[source].astype(F32)

        total = lax.fori_loop(1, chips, collect, part[base + mine] + pair[mine])
        full[base + mine] = (total * scale).astype(BF16)

        def send(i, _):
            gather_copy(lax.rem(chip + i, chips)).start()
            return 0

        lax.fori_loop(1, chips, send, 0)

    def forward_copy(j, side):
        return pltpu.make_async_remote_copy(
            src_ref=full.at[side * count + j], dst_ref=full.at[side * count + j],
            send_sem=fw_s.at[j], recv_sem=fw_r.at[j], device_id=partner, device_id_type=MESH,
        )

    for j in range(count):

        @pl.when(chip != owners[j])
        def _():
            pltpu.make_async_remote_copy(
                src_ref=outbox.at[0], dst_ref=full.at[base + j],
                send_sem=rs_s.at[0], recv_sem=ag_r.at[j], device_id=partner, device_id_type=MESH,
            ).wait_recv()

        forward_copy(j, core).start()
        sum_ref[base + j] = full[base + j]

    for j in range(count):
        forward_copy(j, 1 - core).wait_recv()
        sum_ref[(1 - core) * count + j] = full[(1 - core) * count + j]

    outgoing(lambda copy: copy.wait_send())
    for j in range(count):
        pair_copy(j).wait_send()
        forward_copy(j, core).wait_send()

        @pl.when(chip != owners[j])
        def _():
            scatter_copy(j).wait_send()

    @pl.when(owns)
    def _():
        def sent(i, _):
            gather_copy(lax.rem(chip + i, chips)).wait_send()
            return 0

        lax.fori_loop(1, chips, sent, 0)


def unpack_kernel(sum_ref, out_ref):
    split = out_ref.shape[1] // 2
    rest = out_ref.shape[2] - LANES
    for t in range(out_ref.shape[0]):
        out_ref[t, :split, :LANES] = sum_ref[3 * t].astype(F32)
        out_ref[t, split:, :LANES] = sum_ref[3 * t + 1].astype(F32)
        packed = sum_ref[3 * t + 2].astype(F32)
        out_ref[t, :split, LANES:] = packed[:, :rest]
        out_ref[t, split:, LANES:] = packed[:, rest:]


def per_device(n_rows, n_cols, grad_out, inputs, weight):
    rows_local, cols_local, chans = inputs.shape
    half_rows, half_cols = rows_local // 2, cols_local // 2
    split = chans // 2
    chips = n_rows * n_cols // 2
    count = (27 + 1) // 2
    scale = 1.0 / math.sqrt(half_rows * n_rows * half_cols * n_cols)
    dma = pltpu.SemaphoreType.DMA
    vmem = pl.BlockSpec(memory_space=pltpu.VMEM)
    anywhere = pl.BlockSpec(memory_space=pl.ANY)
    input_grad, sums = pl.pallas_call(
        functools.partial(step_kernel, n_rows, n_cols, scale),
        out_shape=(
            jax.ShapeDtypeStruct(inputs.shape, BF16),
            jax.ShapeDtypeStruct((2 * count, split, LANES), BF16),
        ),
        in_specs=[vmem, anywhere, anywhere],
        out_specs=(vmem, vmem),
        scratch_shapes=[
            pltpu.VMEM(inputs.shape, BF16),
            pltpu.VMEM(weight.shape, BF16),
            pltpu.VMEM((half_rows + 1, half_cols, chans), BF16),
            pltpu.VMEM((half_rows + 1, EDGE, chans), BF16),
            pltpu.VMEM((half_rows + 1, half_cols, chans), BF16),
            pltpu.VMEM((2, 2, chans, half_rows * half_cols), BF16),
            pltpu.VMEM((2 * count, split, LANES), F32),
            pltpu.VMEM((count, split, LANES), F32),
            pltpu.VMEM((count, split, LANES), BF16),
            pltpu.VMEM((chips, split, LANES), BF16),
            pltpu.VMEM((2 * count, split, LANES), BF16),
            dma((2,)),
            dma((n_cols,)), dma((half_rows + 1,)), dma((n_cols,)), dma((half_rows + 1,)), dma((2, n_cols)),
            dma((count,)), dma((count,)),
            dma((count,)), dma((chips,)), dma((chips,)), dma((count,)),
            dma((count,)), dma((count,)),
        ],
        compiler_params=pltpu.CompilerParams(
            collective_id=0, has_side_effects=True, vmem_limit_bytes=48 * 1024 * 1024
        ),
    )(grad_out, inputs, weight)
    filter_grad = pl.pallas_call(
        unpack_kernel,
        grid=(3,),
        out_shape=jax.ShapeDtypeStruct((9, chans, chans), F32),
        in_specs=[pl.BlockSpec((9, split, LANES), lambda i: (i, 0, 0))],
        out_specs=pl.BlockSpec((3, chans, chans), lambda i: (i, 0, 0)),
    )(sums)
    return input_grad, filter_grad.reshape(3, 3, chans, chans)


def solution(mesh):
    in_specs = (P(("rows", "cols"), None, None), P("rows", "cols", None), P())
    out_specs = (P("rows", "cols", None), P())
    return jax.shard_map(
        functools.partial(per_device, mesh.shape["rows"], mesh.shape["cols"]),
        mesh=mesh, in_specs=in_specs, out_specs=out_specs, check_vma=False,
    )
```

time: 209 us -> 42.7 us (0.20)
  the two profiles are of different devices: /device:TPU:1 before, /device:TPU:29 now
where the time goes in v1:
time: 42.7 us; the launch traced here: 42.5 us
  Pallas kernels  37.2 us (87%)
  local copies, waits for them, and re-layouts  4.68 us (11%)
  between operations  0.68 us (2%)
    pallas_call x1, Pallas kernels, per_device(): pl.pallas_call(functools.partial(step_kernel, n_rows, n_cols, scale), out...  34 us
    unnamed x7, local copies, waits for them, and re-layouts  4.68 us
    pallas_call x1, Pallas kernels, per_device(): pl.pallas_call(unpack_kernel, grid=(3,), out_shape=jax.ShapeDtypeStruct((...  3.14 us

profile of v1, /device:TPU:29, one launch (start us, length us, event | category | flops | bytes accessed | tf_op | source)
XLA Modules:
  0.0 42.5 jit_solution(5495135503265317900)
XLA Ops:
  0.6 0.0 copy-start
  0.6 1.1 %copy.5.g_ref = bf16[1,512,192]{2,1,0:T(8,128)(2,1)S(1)} copy(bf16[1,512,192]{1,2,0:T(8,128)(2,1)} %param.3) | data formatting | bytes 393216 | tf_op args[0]
  1.8 1.4 %copy.6.x_hbm = bf16[8,256,192]{2,1,0:T(8,128)(2,1)S(1)} copy(bf16[8,256,192]{1,2,0:T(8,128)(2,1)} %param.4) | data formatting | bytes 1572864 | tf_op args[1]
  3.2 0.0 copy-done
  3.2 34.0 %shard_map.50 = (bf16[8,256,192]{2,1,0:T(8,128)(2,1)S(1)}, bf16[28,96,128]{2,1,0:T(8,128)(2,1)S(1)}) custom-call(bf16[1,512,192]{2,1,0:T(8,128)(2,1)S(1)} %copy.5.g_ref, bf16[8,256,192]{2,1,0:T(8,128)(2,1)S(1)} %copy.6.x_hbm, bf16[3,3,192,192]{3,2,1,0:T(8,128)(2,1)S(1)} %copy-done), custom_call_target="tpu_custom_call" | custom-call | tf_op jit(solution)/shard_map/pallas_call | solution.py:298
  37.3 0.0 copy-start.1
  37.3 0.8 %copy-done.1 = bf16[28,96,128]{2,1,0:T(8,128)(2,1)} copy-done((bf16[28,96,128]{2,1,0:T(8,128)(2,1)}, bf16[28,96,128]{2,1,0:T(8,128)(2,1)S(1)}, u32[]{:S(2)}) %copy-start.1) | copy-done | bytes 688152
  38.1 1.3 %copy.7 = bf16[8,256,192]{1,2,0:T(8,128)(2,1)} copy(bf16[8,256,192]{2,1,0:T(8,128)(2,1)S(1)} %get-tuple-element.6) | data formatting | bytes 1572864
  39.4 3.1 %shard_map.51 = f32[9,192,192]{2,1,0:T(8,128)} custom-call(bf16[28,96,128]{2,1,0:T(8,128)(2,1)} %copy-done.1), custom_call_target="tpu_custom_call" | custom-call | tf_op jit(solution)/shard_map/pallas_call | solution.py:328
Async XLA Ops:
  0.6 2.6 %copy-start = (bf16[3,3,192,192]{3,2,1,0:T(8,128)(2,1)S(1)}, bf16[3,3,192,192]{3,2,1,0:T(8,128)(2,1)}, u32[]{:S(2)}) copy-start(bf16[3,3,192,192]{3,2,1,0:T(8,128)(2,1)} %w_hbm.1) | copy-start | bytes 1990660
  37.3 0.9 %copy-start.1 = (bf16[28,96,128]{2,1,0:T(8,128)(2,1)}, bf16[28,96,128]{2,1,0:T(8,128)(2,1)S(1)}, u32[]{:S(2)}) copy-start(bf16[28,96,128]{2,1,0:T(8,128)(2,1)S(1)} %get-tuple-element.5.sum_ref) | copy-start | bytes 2064388

commit v2 on v1

v2 whole, which is shorter than its diff:
```python
import functools
import math

import jax
import jax.numpy as jnp
from jax import lax
from jax.experimental import pallas as pl
from jax.experimental.pallas import tpu as pltpu
from jax.sharding import PartitionSpec as P

MESH = pl.DeviceIdType.MESH
LANES = 128
EDGE = 16
F32 = jnp.float32
BF16 = jnp.bfloat16
PARITY = (1, 0, 1)
SHIFT = (1, 0, 0)


def iota(shape, dim):
    return lax.broadcasted_iota(jnp.int32, shape, dim)


def ones_where(mask):
    return jnp.where(mask, 1.0, 0.0).astype(BF16)


def spread_matrix(size, back):
    half = size // 2
    i = iota((size, size), 0 if back else 1)
    k = iota((size, size), 1 if back else 0)
    return ones_where(k == jnp.where(i < half, 2 * i, 2 * (i - half) + 1))


def nn(a, b):
    return jnp.dot(a, b, preferred_element_type=F32)


def nt(a, b):
    return lax.dot_general(a, b, (((1,), (1,)), ((), ())), preferred_element_type=F32)


def step_kernel(
    n_rows, n_cols, scale,
    g_ref, x_hbm, w_hbm, ig_ref, sum_ref,
    x, w, gm, gh, gs, edge, xt, part, pair, outbox, inbox, full,
    load_sem, main_s, main_r, halo_s, halo_r, up_s, pair_s, pair_r,
    rs_s, rs_r, ag_s, ag_r, fw_s, fw_r,
):
    r = lax.axis_index("rows")
    c = lax.axis_index("cols")
    core = lax.rem(c, 2)
    depth = n_cols // 2
    chips = n_rows * depth
    chip = r * depth + c // 2
    partner = (r, c + 1 - 2 * core)
    half_rows = n_cols
    half_cols = g_ref.shape[2] // n_cols
    chans = g_ref.shape[1]
    count = outbox.shape[0]
    base = core * count
    devices = n_rows * n_cols
    me = r * n_cols + c

    barrier = pltpu.get_barrier_semaphore()

    def greet(i, _):
        other = lax.rem(me + i, devices)
        pl.semaphore_signal(
            barrier, inc=1, device_id=(other // n_cols, lax.rem(other, n_cols)), device_id_type=MESH
        )
        return 0

    lax.fori_loop(1, devices, greet, 0)
    load_x = pltpu.make_async_copy(x_hbm, x, load_sem.at[0])
    load_w = pltpu.make_async_copy(w_hbm, w, load_sem.at[1])
    load_x.start()
    load_w.start()

    def block(i):
        return slice(i * half_cols, (i + 1) * half_cols)

    @pl.when(r == n_rows - 1)
    def _():
        gm[:, block(half_rows)] = jnp.zeros((chans, half_cols), BF16)
        gh[half_rows] = jnp.zeros(gh.shape[1:], BF16)

    for q in range(n_cols):

        @pl.when(c == q)
        def _():
            gm[:, block(q)] = g_ref[0, :, block(q)]

    full_cols = g_ref.shape[2]
    wanted = (iota((EDGE, full_cols), 0) + 1) * half_cols
    edge[...] = nt(ones_where(wanted == iota((EDGE, full_cols), 1)), g_ref[0]).astype(BF16)
    gh[c] = edge[...]

    pl.semaphore_wait(barrier, devices - 1)

    def main_copy(q, row, slot, send):
        return pltpu.make_async_remote_copy(
            src_ref=g_ref.at[0, :, pl.ds(q * half_cols, half_cols)],
            dst_ref=gm.at[:, pl.ds(pl.multiple_of(slot * half_cols, LANES), half_cols)],
            send_sem=send, recv_sem=main_r.at[slot], device_id=(row, q), device_id_type=MESH,
        )

    def halo_copy(q, row, slot, send):
        return pltpu.make_async_remote_copy(
            src_ref=edge, dst_ref=gh.at[slot],
            send_sem=send, recv_sem=halo_r.at[slot], device_id=(row, q), device_id_type=MESH,
        )

    def outgoing(act):
        for q in range(n_cols):

            @pl.when((c == 0) & (r > 0))
            def _():
                act(main_copy(q, r - 1, half_rows, up_s.at[0, q]))
                act(halo_copy(q, r - 1, half_rows, up_s.at[1, q]))

            @pl.when(c != q)
            def _():
                act(main_copy(q, r, c, main_s.at[q]))
                act(halo_copy(q, r, c, halo_s.at[q]))

    outgoing(lambda copy: copy.start())

    load_x.wait()
    width = x.shape[2]
    sort = spread_matrix(width, False)
    for p in range(x.shape[0]):
        ordered = nn(x[p], sort).astype(BF16)
        for s in range(2):
            xt[p % 2, s, :, block(p // 2)] = ordered[:, block(s)]

    for i in range(half_rows + 1):
        if i < half_rows:
            arrives = c != i
        else:
            arrives = r < n_rows - 1

        @pl.when(arrives)
        def _():
            main_copy(0, r, i, main_s.at[0]).wait_recv()
            halo_copy(0, r, i, halo_s.at[0]).wait_recv()

    slots = half_rows + 1
    eye = ones_where(iota((chans, chans), 0) == iota((chans, chans), 1))
    turned = nt(eye, gh[...].reshape(slots * EDGE, chans)).astype(BF16)
    shift = ones_where(iota((half_cols, half_cols), 0) == iota((half_cols, half_cols), 1) + 1)
    for i in range(slots):
        place = (slots * EDGE, half_cols)
        last = (iota(place, 0) == i * EDGE + c) & (iota(place, 1) == half_cols - 1)
        gs[:, block(i)] = (nn(gm[:, block(i)], shift) + nn(turned, ones_where(last))).astype(BF16)

    def grad(down, along):
        src = gs if along else gm
        return src[:, down * half_cols : (down + half_rows) * half_cols]

    split = chans // 2
    part[2 * count - 1] = jnp.zeros(part.shape[1:], F32)
    for a in range(3):
        for b in range(3):
            t = 3 * a + b
            terms = nt(xt[PARITY[a], PARITY[b]], grad(SHIFT[a], SHIFT[b]))
            part[3 * t] = terms[:split, :LANES]
            part[3 * t + 1] = terms[split:, :LANES]
            part[3 * t + 2] = jnp.concatenate([terms[:split, LANES:], terms[split:, LANES:]], axis=1)

    def pair_copy(j):
        return pltpu.make_async_remote_copy(
            src_ref=part.at[(1 - core) * count + j], dst_ref=pair.at[j],
            send_sem=pair_s.at[j], recv_sem=pair_r.at[j], device_id=partner, device_id_type=MESH,
        )

    upper = chip // (chips // 2)
    half_count = count // 2

    def far_first(i):
        near = i // half_count
        side = upper * near + (1 - upper) * (1 - near)
        return side * half_count + lax.rem(chip + i, half_count)

    def owner_of(j):
        return (j * chips) // count

    for i in range(count):
        pair_copy(far_first(i)).start()

    def scatter_copy(j):
        owner = owner_of(j)
        return pltpu.make_async_remote_copy(
            src_ref=outbox.at[j], dst_ref=inbox.at[chip],
            send_sem=rs_s.at[j], recv_sem=rs_r.at[chip],
            device_id=(owner // depth, 2 * lax.rem(owner, depth) + core), device_id_type=MESH,
        )

    for i in range(count):
        j = far_first(i)
        pair_copy(j).wait_recv()
        outbox[j] = (part[base + j] + pair[j]).astype(BF16)

        @pl.when(chip != owner_of(j))
        def _():
            scatter_copy(j).start()

    load_w.wait()
    back = spread_matrix(width, True)

    def tap(a, b):
        return nn(w[a, b], grad(SHIFT[a], SHIFT[b]))

    for odd in range(2):
        taps = (0, 2) if odd else (1,)
        even_cols = sum(tap(a, 1) for a in taps).astype(BF16)
        odd_cols = sum(tap(a, 0) + tap(a, 2) for a in taps).astype(BF16)
        for i in range(half_rows):
            both = jnp.concatenate([even_cols[:, block(i)], odd_cols[:, block(i)]], axis=1)
            ig_ref[2 * i + odd] = nn(both, back).astype(BF16)

    mine = (chip * count + chips - 1) // chips
    owns = (mine < count) & ((mine * chips) // count == chip)

    def gather_copy(other):
        return pltpu.make_async_remote_copy(
            src_ref=full.at[base + mine], dst_ref=full.at[base + mine],
            send_sem=ag_s.at[other], recv_sem=ag_r.at[mine],
            device_id=(other // depth, 2 * lax.rem(other, depth) + core), device_id_type=MESH,
        )

    @pl.when(owns)
    def _():
        def collect(i, total):
            source = lax.rem(chip + i, chips)
            pltpu.make_async_remote_copy(
                src_ref=outbox.at[0], dst_ref=inbox.at[source],
                send_sem=rs_s.at[0], recv_sem=rs_r.at[source], device_id=partner, device_id_type=MESH,
            ).wait_recv()
            return total + inbox[source].astype(F32)

        total = lax.fori_loop(1, chips, collect, part[base + mine] + pair[mine])
        full[base + mine] = (total * scale).astype(BF16)

        def send(i, _):
            near = i // (chips // 2)
            side = upper * near + (1 - upper) * (1 - near)
            other = side * (chips // 2) + lax.rem(chip + i, chips // 2)

            @pl.when(other != chip)
            def _():
                gather_copy(other).start()

            return 0

        lax.fori_loop(0, chips, send, 0)

    def forward_copy(j, side):
        return pltpu.make_async_remote_copy(
            src_ref=full.at[side * count + j], dst_ref=full.at[side * count + j],
            send_sem=fw_s.at[j], recv_sem=fw_r.at[j], device_id=partner, device_id_type=MESH,
        )

    for j in range(count):

        @pl.when(chip != owner_of(j))
        def _():
            pltpu.make_async_remote_copy(
                src_ref=outbox.at[0], dst_ref=full.at[base + j],
                send_sem=rs_s.at[0], recv_sem=ag_r.at[j], device_id=partner, device_id_type=MESH,
            ).wait_recv()

        forward_copy(j, core).start()
        sum_ref[base + j] = full[base + j]

    for j in range(count):
        forward_copy(j, 1 - core).wait_recv()
        sum_ref[(1 - core) * count + j] = full[(1 - core) * count + j]

    outgoing(lambda copy: copy.wait_send())
    for j in range(count):
        pair_copy(j).wait_send()
        forward_copy(j, core).wait_send()

        @pl.when(chip != owner_of(j))
        def _():
            scatter_copy(j).wait_send()

    @pl.when(owns)
    def _():
        def sent(i, _):
            gather_copy(lax.rem(chip + i, chips)).wait_send()
            return 0

        lax.fori_loop(1, chips, sent, 0)


def unpack_kernel(ig_ref, sum_ref, ig_out, filter_out, wide, sems):
    split = wide.shape[1] // 2
    rest = wide.shape[2] - LANES
    taps = wide.shape[0]
    whole = pltpu.make_async_copy(ig_ref, ig_out, sems.at[taps])
    whole.start()
    copies = []
    for t in range(taps):
        wide[t, :split, :LANES] = sum_ref[3 * t].astype(F32)
        wide[t, split:, :LANES] = sum_ref[3 * t + 1].astype(F32)
        packed = sum_ref[3 * t + 2].astype(F32)
        wide[t, :split, LANES:] = packed[:, :rest]
        wide[t, split:, LANES:] = packed[:, rest:]
        copies.append(pltpu.make_async_copy(wide.at[t], filter_out.at[t], sems.at[t]))
        copies[-1].start()
    whole.wait()
    for copy in copies:
        copy.wait()


def per_device(n_rows, n_cols, grad_out, inputs, weight):
    rows_local, cols_local, chans = inputs.shape
    grad_out, inputs = (jnp.swapaxes(grad_out, 1, 2), jnp.swapaxes(inputs, 1, 2))
    half_rows, half_cols = rows_local // 2, cols_local // 2
    split = chans // 2
    chips = n_rows * n_cols // 2
    count = (27 + 1) // 2
    scale = 1.0 / math.sqrt(half_rows * n_rows * half_cols * n_cols)
    dma = pltpu.SemaphoreType.DMA
    vmem = pl.BlockSpec(memory_space=pltpu.VMEM)
    anywhere = pl.BlockSpec(memory_space=pl.ANY)
    hbm = pl.BlockSpec(memory_space=pltpu.HBM)
    input_grad, sums = pl.pallas_call(
        functools.partial(step_kernel, n_rows, n_cols, scale),
        out_shape=(
            jax.ShapeDtypeStruct(inputs.shape, BF16),
            jax.ShapeDtypeStruct((2 * count, split, LANES), BF16),
        ),
        in_specs=[vmem, hbm, hbm],
        out_specs=(vmem, vmem),
        scratch_shapes=[
            pltpu.VMEM(inputs.shape, BF16),
            pltpu.VMEM(weight.shape, BF16),
            pltpu.VMEM((chans, (half_rows + 1) * half_cols), BF16),
            pltpu.VMEM((half_rows + 1, EDGE, chans), BF16),
            pltpu.VMEM((chans, (half_rows + 1) * half_cols), BF16),
            pltpu.VMEM((EDGE, chans), BF16),
            pltpu.VMEM((2, 2, chans, half_rows * half_cols), BF16),
            pltpu.VMEM((2 * count, split, LANES), F32),
            pltpu.VMEM((count, split, LANES), F32),
            pltpu.VMEM((count, split, LANES), BF16),
            pltpu.VMEM((chips, split, LANES), BF16),
            pltpu.VMEM((2 * count, split, LANES), BF16),
            dma((2,)),
            dma((n_cols,)), dma((half_rows + 1,)), dma((n_cols,)), dma((half_rows + 1,)), dma((2, n_cols)),
            dma((count,)), dma((count,)),
            dma((count,)), dma((chips,)), dma((chips,)), dma((count,)),
            dma((count,)), dma((count,)),
        ],
        compiler_params=pltpu.CompilerParams(
            collective_id=0, has_side_effects=True, vmem_limit_bytes=48 * 1024 * 1024
        ),
    )(grad_out, inputs, weight)
    input_grad, filter_grad = pl.pallas_call(
        unpack_kernel,
        out_shape=(
            jax.ShapeDtypeStruct(inputs.shape, BF16),
            jax.ShapeDtypeStruct((9, chans, chans), F32),
        ),
        in_specs=[vmem, vmem],
        out_specs=(anywhere, anywhere),
        scratch_shapes=[pltpu.VMEM((9, chans, chans), F32), dma((10,))],
        compiler_params=pltpu.CompilerParams(vmem_limit_bytes=12 * 1024 * 1024),
    )(input_grad, sums)
    return jnp.swapaxes(input_grad, 1, 2), filter_grad.reshape(3, 3, chans, chans)


def solution(mesh):
    in_specs = (P(("rows", "cols"), None, None), P("rows", "cols", None), P())
    out_specs = (P("rows", "cols", None), P())
    return jax.shard_map(
        functools.partial(per_device, mesh.shape["rows"], mesh.shape["cols"]),
        mesh=mesh, in_specs=in_specs, out_specs=out_specs, check_vma=False,
    )
```

time: 42.7 us -> 40.5 us (0.948)
  the two profiles are of different devices: /device:TPU:29 before, /device:TPU:1 now
where the time goes in v2:
time: 40.5 us; the launch traced here: 40.3 us
  Pallas kernels  36.4 us (90%)
  local copies, waits for them, and re-layouts  3.22 us (8%)
  between operations  0.65 us (2%)
    pallas_call x1, Pallas kernels, per_device(): pl.pallas_call(functools.partial(step_kernel, n_rows, n_cols, scale), out...  34.9 us
    unnamed x6, local copies, waits for them, and re-layouts  3.22 us
    pallas_call x1, Pallas kernels, per_device(): pl.pallas_call(unpack_kernel, out_shape=(jax.ShapeDtypeStruct(inputs.shap...  1.54 us

profile of v2, /device:TPU:1, one launch (start us, length us, event | category | flops | bytes accessed | tf_op | source)
XLA Modules:
  0.0 40.3 jit_solution(8705576629794704337)
XLA Ops:
  0.6 0.0 copy-start
  0.6 1.2 %copy-done = bf16[3,3,192,192]{3,2,1,0:T(8,128)(2,1)S(1)} copy-done((bf16[3,3,192,192]{3,2,1,0:T(8,128)(2,1)S(1)}, bf16[3,3,192,192]{3,2,1,0:T(8,128)(2,1)}, u32[]{:S(2)}) %copy-start) | copy-done | bytes 663576
  1.8 0.0 copy-start.1
  1.8 1.1 %copy-done.1 = bf16[8,256,192]{1,2,0:T(8,128)(2,1)S(1)} copy-done((bf16[8,256,192]{1,2,0:T(8,128)(2,1)S(1)}, bf16[8,256,192]{1,2,0:T(8,128)(2,1)}, u32[]{:S(2)}) %copy-start.1) | copy-done | bytes 786456
  2.9 0.0 copy-start.2
  2.9 0.9 %copy-done.2 = bf16[1,512,192]{1,2,0:T(8,128)(2,1)S(1)} copy-done((bf16[1,512,192]{1,2,0:T(8,128)(2,1)S(1)}, bf16[1,512,192]{1,2,0:T(8,128)(2,1)}, u32[]{:S(2)}) %copy-start.2) | copy-done | bytes 196632
  3.9 34.9 %shard_map.50 = (bf16[8,192,256]{2,1,0:T(8,128)(2,1)S(1)}, bf16[28,96,128]{2,1,0:T(8,128)(2,1)S(1)}) custom-call(bf16[1,192,512]{2,1,0:T(8,128)(2,1)S(1)} %bitcast.5, bf16[8,192,256]{2,1,0:T(8,128)(2,1)S(1)} %bitcast.4, bf16[3,3,192,192]{3,2,1,0:T(8,128)(2,1)S(1)} %copy-done), custom_call_target="tpu_custom_call" | custom-call | tf_op jit(solution)/shard_map/pallas_call | solution.py:330
  38.7 1.5 %shard_map.51 = (bf16[8,192,256]{2,1,0:T(8,128)(2,1)}, f32[9,192,192]{2,1,0:T(8,128)}) custom-call(bf16[8,192,256]{2,1,0:T(8,128)(2,1)S(1)} %get-tuple-element.6.ig_ref, bf16[28,96,128]{2,1,0:T(8,128)(2,1)S(1)} %get-tuple-element.7.sum_ref), custom_call_target="tpu_custom_call" | custom-call | tf_op jit(solution)/shard_map/pallas_call | solution.py:361
Async XLA Ops:
  0.6 1.2 %copy-start = (bf16[3,3,192,192]{3,2,1,0:T(8,128)(2,1)S(1)}, bf16[3,3,192,192]{3,2,1,0:T(8,128)(2,1)}, u32[]{:S(2)}) copy-start(bf16[3,3,192,192]{3,2,1,0:T(8,128)(2,1)} %w_hbm.1) | copy-start | bytes 1990660
  1.8 1.1 %copy-start.1 = (bf16[8,256,192]{1,2,0:T(8,128)(2,1)S(1)}, bf16[8,256,192]{1,2,0:T(8,128)(2,1)}, u32[]{:S(2)}) copy-start(bf16[8,256,192]{1,2,0:T(8,128)(2,1)} %param.4) | copy-start | bytes 2359300
  2.9 0.9 %copy-start.2 = (bf16[1,512,192]{1,2,0:T(8,128)(2,1)S(1)}, bf16[1,512,192]{1,2,0:T(8,128)(2,1)}, u32[]{:S(2)}) copy-start(bf16[1,512,192]{1,2,0:T(8,128)(2,1)} %param.3) | copy-start | bytes 589828

commit v3 on v2

--- a/solution.py
+++ b/solution.py
@@ -45,7 +45,7 @@
     g_ref, x_hbm, w_hbm, ig_ref, sum_ref,
     x, w, gm, gh, gs, edge, xt, part, pair, outbox, inbox, full,
     load_sem, main_s, main_r, halo_s, halo_r, up_s, pair_s, pair_r,
-    rs_s, rs_r, ag_s, ag_r, fw_s, fw_r,
+    rs_s, rs_r, ag_s, ag_r, plane_s, fw_s, fw_r,
 ):
     r = lax.axis_index("rows")
     c = lax.axis_index("cols")
@@ -219,17 +219,54 @@
             both = jnp.concatenate([even_cols[:, block(i)], odd_cols[:, block(i)]], axis=1)
             ig_ref[2 * i + odd] = nn(both, back).astype(BF16)
 
-    mine = (chip * count + chips - 1) // chips
-    owns = (mine < count) & ((mine * chips) // count == chip)
-
-    def gather_copy(other):
-        return pltpu.make_async_remote_copy(
-            src_ref=full.at[base + mine], dst_ref=full.at[base + mine],
-            send_sem=ag_s.at[other], recv_sem=ag_r.at[mine],
-            device_id=(other // depth, 2 * lax.rem(other, depth) + core), device_id_type=MESH,
-        )
-
-    @pl.when(owns)
+    plane = 2 * depth
+    layers = chips // plane
+    layer, spot = chip // plane, lax.rem(chip, plane)
+
+    def chunk_of(other):
+        return (other * count + chips - 1) // chips
+
+    def owns(other):
+        return (chunk_of(other) < count) & (owner_of(chunk_of(other)) == other)
+
+    mine = chunk_of(chip)
+
+    def share(j, row, col, send):
+        return pltpu.make_async_remote_copy(
+            src_ref=full.at[base + j], dst_ref=full.at[base + j],
+            send_sem=send, recv_sem=ag_r.at[j], device_id=(row, col), device_id_type=MESH,
+        )
+
+    def to_layers(act):
+        @pl.when(owns(chip))
+        def _():
+            for i in range(layers):
+                other = lax.rem(layer + i + layers // 2, layers)
+
+                @pl.when(other != layer)
+                def _():
+                    act(share(mine, 2 * other + spot // depth, c, ag_s.at[other]))
+
+    def to_plane(source_layer, act):
+        j = chunk_of(source_layer * plane + spot)
+        for i in range(1, plane):
+            other = lax.rem(spot + i, plane)
+            act(share(
+                j, 2 * layer + other // depth, 2 * lax.rem(other, depth) + core,
+                plane_s.at[source_layer, other],
+            ))
+
+    def forward_copy(j, side):
+        return pltpu.make_async_remote_copy(
+            src_ref=full.at[side * count + j], dst_ref=full.at[side * count + j],
+            send_sem=fw_s.at[j], recv_sem=fw_r.at[j], device_id=partner, device_id_type=MESH,
+        )
+
+    def pass_on(j):
+        forward_copy(j, core).start()
+        sum_ref[base + j] = full[base + j]
+
+    @pl.when(owns(chip))
     def _():
         def collect(i, total):
             source = lax.rem(chip + i, chips)
@@ -242,36 +279,40 @@
         total = lax.fori_loop(1, chips, collect, part[base + mine] + pair[mine])
         full[base + mine] = (total * scale).astype(BF16)
 
-        def send(i, _):
-            near = i // (chips // 2)
-            side = upper * near + (1 - upper) * (1 - near)
-            other = side * (chips // 2) + lax.rem(chip + i, chips // 2)
-
-            @pl.when(other != chip)
-            def _():
-                gather_copy(other).start()
-
-            return 0
-
-        lax.fori_loop(0, chips, send, 0)
-
-    def forward_copy(j, side):
-        return pltpu.make_async_remote_copy(
-            src_ref=full.at[side * count + j], dst_ref=full.at[side * count + j],
-            send_sem=fw_s.at[j], recv_sem=fw_r.at[j], device_id=partner, device_id_type=MESH,
-        )
-
-    for j in range(count):
-
-        @pl.when(chip != owner_of(j))
-        def _():
-            pltpu.make_async_remote_copy(
-                src_ref=outbox.at[0], dst_ref=full.at[base + j],
-                send_sem=rs_s.at[0], recv_sem=ag_r.at[j], device_id=partner, device_id_type=MESH,
-            ).wait_recv()
-
-        forward_copy(j, core).start()
-        sum_ref[base + j] = full[base + j]
+    to_layers(lambda copy: copy.start())
+
+    @pl.when(owns(chip))
+    def _():
+        to_plane(layer, lambda copy: copy.start())
+        pass_on(mine)
+
+    def relay(i, _):
+        source_layer = lax.rem(layer + i, layers)
+        source = source_layer * plane + spot
+
+        @pl.when(owns(source))
+        def _():
+            share(chunk_of(source), r, c, ag_s.at[layer]).wait_recv()
+            to_plane(source_layer, lambda copy: copy.start())
+            pass_on(chunk_of(source))
+
+        return 0
+
+    lax.fori_loop(1, layers, relay, 0)
+
+    def take(i, _):
+        source = lax.rem(layer + i // (plane - 1), layers) * plane + lax.rem(
+            spot + 1 + lax.rem(i, plane - 1), plane
+        )
+
+        @pl.when(owns(source))
+        def _():
+            share(chunk_of(source), r, c, ag_s.at[layer]).wait_recv()
+            pass_on(chunk_of(source))
+
+        return 0
+
+    lax.fori_loop(0, layers * (plane - 1), take, 0)
 
     for j in range(count):
         forward_copy(j, 1 - core).wait_recv()
@@ -286,13 +327,16 @@
         def _():
             scatter_copy(j).wait_send()
 
-    @pl.when(owns)
-    def _():
-        def sent(i, _):
-            gather_copy(lax.rem(chip + i, chips)).wait_send()
-            return 0
-
-        lax.fori_loop(1, chips, sent, 0)
+    to_layers(lambda copy: copy.wait_send())
+
+    def sent(i, _):
+        @pl.when(owns(i * plane + spot))
+        def _():
+            to_plane(i, lambda copy: copy.wait_send())
+
+        return 0
+
+    lax.fori_loop(0, layers, sent, 0)
 
 
 def unpack_kernel(ig_ref, sum_ref, ig_out, filter_out, wide, sems):
@@ -318,6 +362,8 @@
 def per_device(n_rows, n_cols, grad_out, inputs, weight):
     rows_local, cols_local, chans = inputs.shape
     grad_out, inputs = (jnp.swapaxes(grad_out, 1, 2), jnp.swapaxes(inputs, 1, 2))
+    inputs = pltpu.with_memory_space_constraint(inputs, pltpu.HBM)
+    weight = pltpu.with_memory_space_constraint(weight, pltpu.HBM)
     half_rows, half_cols = rows_local // 2, cols_local // 2
     split = chans // 2
     chips = n_rows * n_cols // 2
@@ -351,7 +397,7 @@
             dma((2,)),
             dma((n_cols,)), dma((half_rows + 1,)), dma((n_cols,)), dma((half_rows + 1,)), dma((2, n_cols)),
             dma((count,)), dma((count,)),
-            dma((count,)), dma((chips,)), dma((chips,)), dma((count,)),
+            dma((count,)), dma((chips,)), dma((chips,)), dma((count,)), dma((chips // n_cols, n_cols)),
             dma((count,)), dma((count,)),
         ],
         compiler_params=pltpu.CompilerParams(

time: 40.5 us -> 36.7 us (0.906)
  local copies, waits for them, and re-layouts: 3.22 us -> 0.92 us
  Pallas kernels: 36.4 us -> 35 us
    unnamed x6 -> x2, local copies, waits for them, and re-layouts: 3.22 us -> 0.92 us
    pallas_call x1, Pallas kernels: 34.9 us -> 33.4 us  [per_device(): pl.pallas_call(functools.partial(step_kernel, n_rows, n_cols, scale), out...]
where the time goes in v3:
time: 36.7 us; the launch traced here: 36.5 us
  Pallas kernels  35 us (95%)
  local copies, waits for them, and re-layouts  0.92 us (3%)
  between operations  0.65 us (2%)
    pallas_call x1, Pallas kernels, per_device(): pl.pallas_call(functools.partial(step_kernel, n_rows, n_cols, scale), out...  33.4 us
    pallas_call x1, Pallas kernels, per_device(): pl.pallas_call(unpack_kernel, out_shape=(jax.ShapeDtypeStruct(inputs.shap...  1.54 us
    unnamed x2, local copies, waits for them, and re-layouts  0.92 us

profile of v3, /device:TPU:1, one launch (start us, length us, event | category | flops | bytes accessed | tf_op | source)
XLA Modules:
  0.0 36.5 jit_solution(3576313290870661657)
XLA Ops:
  0.6 0.0 copy-start
  0.6 0.9 %copy-done = bf16[1,512,192]{1,2,0:T(8,128)(2,1)S(1)} copy-done((bf16[1,512,192]{1,2,0:T(8,128)(2,1)S(1)}, bf16[1,512,192]{1,2,0:T(8,128)(2,1)}, u32[]{:S(2)}) %copy-start) | copy-done | bytes 196632
  1.6 33.4 %shard_map.50 = (bf16[8,192,256]{2,1,0:T(8,128)(2,1)S(1)}, bf16[28,96,128]{2,1,0:T(8,128)(2,1)S(1)}) custom-call(bf16[1,192,512]{2,1,0:T(8,128)(2,1)S(1)} %bitcast.4, bf16[8,192,256]{2,1,0:T(8,128)(2,1)} %bitcast.5, bf16[3,3,192,192]{3,2,1,0:T(8,128)(2,1)} %w_hbm.1), custom_call_target="tpu_custom_call" | custom-call | tf_op jit(solution)/shard_map/pallas_call | solution.py:376
  35.0 1.5 %shard_map.51 = (bf16[8,192,256]{2,1,0:T(8,128)(2,1)}, f32[9,192,192]{2,1,0:T(8,128)}) custom-call(bf16[8,192,256]{2,1,0:T(8,128)(2,1)S(1)} %get-tuple-element.6.ig_ref, bf16[28,96,128]{2,1,0:T(8,128)(2,1)S(1)} %get-tuple-element.7.sum_ref), custom_call_target="tpu_custom_call" | custom-call | tf_op jit(solution)/shard_map/pallas_call | solution.py:407
Async XLA Ops:
  0.6 0.9 %copy-start = (bf16[1,512,192]{1,2,0:T(8,128)(2,1)S(1)}, bf16[1,512,192]{1,2,0:T(8,128)(2,1)}, u32[]{:S(2)}) copy-start(bf16[1,512,192]{1,2,0:T(8,128)(2,1)} %param.3) | copy-start | bytes 589828

commit v4 on v3

--- a/solution.py
+++ b/solution.py
@@ -11,6 +11,7 @@
 MESH = pl.DeviceIdType.MESH
 LANES = 128
 EDGE = 16
+PIECES = 2
 F32 = jnp.float32
 BF16 = jnp.bfloat16
 PARITY = (1, 0, 1)
@@ -42,8 +43,8 @@
 
 def step_kernel(
     n_rows, n_cols, scale,
-    g_ref, x_hbm, w_hbm, ig_ref, sum_ref,
-    x, w, gm, gh, gs, edge, xt, part, pair, outbox, inbox, full,
+    g_hbm, x_hbm, w_hbm, ig_ref, sum_ref,
+    g_ref, x, w, gm, gh, gs, edge, xt, part, pair, outbox, inbox, full,
     load_sem, main_s, main_r, halo_s, halo_r, up_s, pair_s, pair_r,
     rs_s, rs_r, ag_s, ag_r, plane_s, fw_s, fw_r,
 ):
@@ -74,6 +75,8 @@
     lax.fori_loop(1, devices, greet, 0)
     load_x = pltpu.make_async_copy(x_hbm, x, load_sem.at[0])
     load_w = pltpu.make_async_copy(w_hbm, w, load_sem.at[1])
+    load_g = pltpu.make_async_copy(g_hbm, g_ref, load_sem.at[2])
+    load_g.start()
     load_x.start()
     load_w.start()
 
@@ -85,6 +88,7 @@
         gm[:, block(half_rows)] = jnp.zeros((chans, half_cols), BF16)
         gh[half_rows] = jnp.zeros(gh.shape[1:], BF16)
 
+    load_g.wait()
     for q in range(n_cols):
 
         @pl.when(c == q)
@@ -188,11 +192,16 @@
     for i in range(count):
         pair_copy(far_first(i)).start()
 
-    def scatter_copy(j):
+    piece = outbox.shape[1] // PIECES
+
+    def cut(h):
+        return pl.ds(h * piece, piece)
+
+    def scatter_copy(j, h):
         owner = owner_of(j)
         return pltpu.make_async_remote_copy(
-            src_ref=outbox.at[j], dst_ref=inbox.at[chip],
-            send_sem=rs_s.at[j], recv_sem=rs_r.at[chip],
+            src_ref=outbox.at[j, cut(h)], dst_ref=inbox.at[chip, cut(h)],
+            send_sem=rs_s.at[h, j], recv_sem=rs_r.at[h, chip],
             device_id=(owner // depth, 2 * lax.rem(owner, depth) + core), device_id_type=MESH,
         )
 
@@ -203,7 +212,15 @@
 
         @pl.when(chip != owner_of(j))
         def _():
-            scatter_copy(j).start()
+            scatter_copy(j, 0).start()
+
+    for h in range(1, PIECES):
+        for i in range(count):
+            j = far_first(i)
+
+            @pl.when(chip != owner_of(j))
+            def _():
+                scatter_copy(j, h).start()
 
     load_w.wait()
     back = spread_matrix(width, True)
@@ -231,13 +248,13 @@
 
     mine = chunk_of(chip)
 
-    def share(j, row, col, send):
-        return pltpu.make_async_remote_copy(
-            src_ref=full.at[base + j], dst_ref=full.at[base + j],
-            send_sem=send, recv_sem=ag_r.at[j], device_id=(row, col), device_id_type=MESH,
-        )
-
-    def to_layers(act):
+    def share(j, h, row, col, send):
+        return pltpu.make_async_remote_copy(
+            src_ref=full.at[base + j, cut(h)], dst_ref=full.at[base + j, cut(h)],
+            send_sem=send, recv_sem=ag_r.at[h, j], device_id=(row, col), device_id_type=MESH,
+        )
+
+    def to_layers(h, act):
         @pl.when(owns(chip))
         def _():
             for i in range(layers):
@@ -245,98 +262,114 @@
 
                 @pl.when(other != layer)
                 def _():
-                    act(share(mine, 2 * other + spot // depth, c, ag_s.at[other]))
-
-    def to_plane(source_layer, act):
+                    act(share(mine, h, 2 * other + spot // depth, c, ag_s.at[h, other]))
+
+    def to_plane(source_layer, h, act):
         j = chunk_of(source_layer * plane + spot)
         for i in range(1, plane):
             other = lax.rem(spot + i, plane)
             act(share(
-                j, 2 * layer + other // depth, 2 * lax.rem(other, depth) + core,
-                plane_s.at[source_layer, other],
+                j, h, 2 * layer + other // depth, 2 * lax.rem(other, depth) + core,
+                plane_s.at[h, source_layer, other],
             ))
 
-    def forward_copy(j, side):
-        return pltpu.make_async_remote_copy(
-            src_ref=full.at[side * count + j], dst_ref=full.at[side * count + j],
-            send_sem=fw_s.at[j], recv_sem=fw_r.at[j], device_id=partner, device_id_type=MESH,
-        )
-
-    def pass_on(j):
-        forward_copy(j, core).start()
-        sum_ref[base + j] = full[base + j]
-
-    @pl.when(owns(chip))
-    def _():
-        def collect(i, total):
-            source = lax.rem(chip + i, chips)
-            pltpu.make_async_remote_copy(
-                src_ref=outbox.at[0], dst_ref=inbox.at[source],
-                send_sem=rs_s.at[0], recv_sem=rs_r.at[source], device_id=partner, device_id_type=MESH,
-            ).wait_recv()
-            return total + inbox[source].astype(F32)
-
-        total = lax.fori_loop(1, chips, collect, part[base + mine] + pair[mine])
-        full[base + mine] = (total * scale).astype(BF16)
-
-    to_layers(lambda copy: copy.start())
-
-    @pl.when(owns(chip))
-    def _():
-        to_plane(layer, lambda copy: copy.start())
-        pass_on(mine)
-
-    def relay(i, _):
-        source_layer = lax.rem(layer + i, layers)
-        source = source_layer * plane + spot
-
-        @pl.when(owns(source))
-        def _():
-            share(chunk_of(source), r, c, ag_s.at[layer]).wait_recv()
-            to_plane(source_layer, lambda copy: copy.start())
-            pass_on(chunk_of(source))
-
-        return 0
-
-    lax.fori_loop(1, layers, relay, 0)
-
-    def take(i, _):
-        source = lax.rem(layer + i // (plane - 1), layers) * plane + lax.rem(
-            spot + 1 + lax.rem(i, plane - 1), plane
-        )
-
-        @pl.when(owns(source))
-        def _():
-            share(chunk_of(source), r, c, ag_s.at[layer]).wait_recv()
-            pass_on(chunk_of(source))
-
-        return 0
-
-    lax.fori_loop(0, layers * (plane - 1), take, 0)
-
-    for j in range(count):
-        forward_copy(j, 1 - core).wait_recv()
-        sum_ref[(1 - core) * count + j] = full[(1 - core) * count + j]
+    def forward_copy(j, h, side):
+        return pltpu.make_async_remote_copy(
+            src_ref=full.at[side * count + j, cut(h)], dst_ref=full.at[side * count + j, cut(h)],
+            send_sem=fw_s.at[h, j], recv_sem=fw_r.at[h, j], device_id=partner, device_id_type=MESH,
+        )
+
+    def pass_on(j, h):
+        forward_copy(j, h, core).start()
+        sum_ref[base + j, cut(h)] = full[base + j, cut(h)]
+
+    def reduce(h):
+        @pl.when(owns(chip))
+        def _():
+            def collect(i, total):
+                source = lax.rem(chip + i, chips)
+                pltpu.make_async_remote_copy(
+                    src_ref=outbox.at[0, cut(h)], dst_ref=inbox.at[source, cut(h)],
+                    send_sem=rs_s.at[h, 0], recv_sem=rs_r.at[h, source],
+                    device_id=partner, device_id_type=MESH,
+                ).wait_recv()
+                return total + inbox[source, cut(h)].astype(F32)
+
+            own = part[base + mine, cut(h)] + pair[mine, cut(h)]
+            total = lax.fori_loop(1, chips, collect, own)
+            full[base + mine, cut(h)] = (total * scale).astype(BF16)
+
+        to_layers(h, lambda copy: copy.start())
+
+        @pl.when(owns(chip))
+        def _():
+            to_plane(layer, h, lambda copy: copy.start())
+            pass_on(mine, h)
+
+    def relay(h):
+        def step(i, _):
+            source_layer = lax.rem(layer + i, layers)
+            source = source_layer * plane + spot
+
+            @pl.when(owns(source))
+            def _():
+                share(chunk_of(source), h, r, c, ag_s.at[h, layer]).wait_recv()
+                to_plane(source_layer, h, lambda copy: copy.start())
+                pass_on(chunk_of(source), h)
+
+            return 0
+
+        lax.fori_loop(1, layers, step, 0)
+
+    def take(h):
+        def step(i, _):
+            source = lax.rem(layer + i // (plane - 1), layers) * plane + lax.rem(
+                spot + 1 + lax.rem(i, plane - 1), plane
+            )
+
+            @pl.when(owns(source))
+            def _():
+                share(chunk_of(source), h, r, c, ag_s.at[h, layer]).wait_recv()
+                pass_on(chunk_of(source), h)
+
+            return 0
+
+        lax.fori_loop(0, layers * (plane - 1), step, 0)
+
+    reduce(0)
+    for h in range(PIECES):
+        relay(h)
+        if h + 1 < PIECES:
+            reduce(h + 1)
+        take(h)
+
+    for h in range(PIECES):
+        for j in range(count):
+            forward_copy(j, h, 1 - core).wait_recv()
+            sum_ref[(1 - core) * count + j, cut(h)] = full[(1 - core) * count + j, cut(h)]
 
     outgoing(lambda copy: copy.wait_send())
     for j in range(count):
         pair_copy(j).wait_send()
-        forward_copy(j, core).wait_send()
-
-        @pl.when(chip != owner_of(j))
-        def _():
-            scatter_copy(j).wait_send()
-
-    to_layers(lambda copy: copy.wait_send())
-
-    def sent(i, _):
-        @pl.when(owns(i * plane + spot))
-        def _():
-            to_plane(i, lambda copy: copy.wait_send())
-
-        return 0
-
-    lax.fori_loop(0, layers, sent, 0)
+
+    for h in range(PIECES):
+        for j in range(count):
+            forward_copy(j, h, core).wait_send()
+
+            @pl.when(chip != owner_of(j))
+            def _():
+                scatter_copy(j, h).wait_send()
+
+        to_layers(h, lambda copy: copy.wait_send())
+
+        def sent(i, _):
+            @pl.when(owns(i * plane + spot))
+            def _():
+                to_plane(i, h, lambda copy: copy.wait_send())
+
+            return 0
+
+        lax.fori_loop(0, layers, sent, 0)
 
 
 def unpack_kernel(ig_ref, sum_ref, ig_out, filter_out, wide, sems):
@@ -362,6 +395,7 @@
 def per_device(n_rows, n_cols, grad_out, inputs, weight):
     rows_local, cols_local, chans = inputs.shape
     grad_out, inputs = (jnp.swapaxes(grad_out, 1, 2), jnp.swapaxes(inputs, 1, 2))
+    grad_out = pltpu.with_memory_space_constraint(grad_out, pltpu.HBM)
     inputs = pltpu.with_memory_space_constraint(inputs, pltpu.HBM)
     weight = pltpu.with_memory_space_constraint(weight, pltpu.HBM)
     half_rows, half_cols = rows_local // 2, cols_local // 2
@@ -379,9 +413,10 @@
             jax.ShapeDtypeStruct(inputs.shape, BF16),
             jax.ShapeDtypeStruct((2 * count, split, LANES), BF16),
         ),
-        in_specs=[vmem, hbm, hbm],
+        in_specs=[hbm, hbm, hbm],
         out_specs=(vmem, vmem),
         scratch_shapes=[
+            pltpu.VMEM(grad_out.shape, BF16),
             pltpu.VMEM(inputs.shape, BF16),
             pltpu.VMEM(weight.shape, BF16),
             pltpu.VMEM((chans, (half_rows + 1) * half_cols), BF16),
@@ -394,11 +429,11 @@
             pltpu.VMEM((count, split, LANES), BF16),
             pltpu.VMEM((chips, split, LANES), BF16),
             pltpu.VMEM((2 * count, split, LANES), BF16),
-            dma((2,)),
+            dma((3,)),
             dma((n_cols,)), dma((half_rows + 1,)), dma((n_cols,)), dma((half_rows + 1,)), dma((2, n_cols)),
             dma((count,)), dma((count,)),
-            dma((count,)), dma((chips,)), dma((chips,)), dma((count,)), dma((chips // n_cols, n_cols)),
-            dma((count,)), dma((count,)),
+            dma((PIECES, count)), dma((PIECES, chips)), dma((PIECES, chips)), dma((PIECES, count)),
+            dma((PIECES, chips // n_cols, n_cols)), dma((PIECES, count)), dma((PIECES, count)),
         ],
         compiler_params=pltpu.CompilerParams(
             collective_id=0, has_side_effects=True, vmem_limit_bytes=48 * 1024 * 1024

time: 36.7 us -> 39.4 us (1.074)
  Pallas kernels: 35 us -> 38.6 us
  local copies, waits for them, and re-layouts: 0.92 us -> 0 us
    pallas_call x1, Pallas kernels: 33.4 us -> 37 us  [per_device(): pl.pallas_call(functools.partial(step_kernel, n_rows, n_cols, scale), out...]
    unnamed x2 -> x0, local copies, waits for them, and re-layouts: 0.92 us -> none
where the time goes in v4:
time: 39.4 us; the launch traced here: 39.2 us
  Pallas kernels  38.6 us (98%)
  between operations  0.64 us (2%)
    pallas_call x1, Pallas kernels, per_device(): pl.pallas_call(functools.partial(step_kernel, n_rows, n_cols, scale), out...  37 us
    pallas_call x1, Pallas kernels, per_device(): pl.pallas_call(unpack_kernel, out_shape=(jax.ShapeDtypeStruct(inputs.shap...  1.54 us

profile of v4, /device:TPU:1, one launch (start us, length us, event | category | flops | bytes accessed | tf_op | source)
XLA Modules:
  0.0 39.2 jit_solution(11625595612025235084)
XLA Ops:
  0.6 37.0 %shard_map.50 = (bf16[8,192,256]{2,1,0:T(8,128)(2,1)S(1)}, bf16[28,96,128]{2,1,0:T(8,128)(2,1)S(1)}) custom-call(bf16[1,192,512]{2,1,0:T(8,128)(2,1)} %bitcast.5, bf16[8,192,256]{2,1,0:T(8,128)(2,1)} %bitcast.4, bf16[3,3,192,192]{3,2,1,0:T(8,128)(2,1)} %w_hbm.1), custom_call_target="tpu_custom_call" | custom-call | tf_op jit(solution)/shard_map/pallas_call | solution.py:410
  37.7 1.5 %shard_map.51 = (bf16[8,192,256]{2,1,0:T(8,128)(2,1)}, f32[9,192,192]{2,1,0:T(8,128)}) custom-call(bf16[8,192,256]{2,1,0:T(8,128)(2,1)S(1)} %get-tuple-element.6.ig_ref, bf16[28,96,128]{2,1,0:T(8,128)(2,1)S(1)} %get-tuple-element.7.sum_ref), custom_call_target="tpu_custom_call" | custom-call | tf_op jit(solution)/shard_map/pallas_call | solution.py:442

commit v5 on v4

--- a/solution.py
+++ b/solution.py
@@ -11,7 +11,7 @@
 MESH = pl.DeviceIdType.MESH
 LANES = 128
 EDGE = 16
-PIECES = 2
+PIECES = 1
 F32 = jnp.float32
 BF16 = jnp.bfloat16
 PARITY = (1, 0, 1)
@@ -258,7 +258,7 @@
         @pl.when(owns(chip))
         def _():
             for i in range(layers):
-                other = lax.rem(layer + i + layers // 2, layers)
+                other = lax.rem(layer + i, layers)
 
                 @pl.when(other != layer)
                 def _():

time: 39.4 us -> 35.6 us (0.904)
  Pallas kernels: 38.6 us -> 34.8 us
    pallas_call x1, Pallas kernels: 37 us -> 33.3 us  [per_device(): pl.pallas_call(functools.partial(step_kernel, n_rows, n_cols, scale), out...]
where the time goes in v5:
time: 35.6 us; the launch traced here: 35.5 us
  Pallas kernels  34.8 us (98%)
  between operations  0.64 us (2%)
    pallas_call x1, Pallas kernels, per_device(): pl.pallas_call(functools.partial(step_kernel, n_rows, n_cols, scale), out...  33.3 us
    pallas_call x1, Pallas kernels, per_device(): pl.pallas_call(unpack_kernel, out_shape=(jax.ShapeDtypeStruct(inputs.shap...  1.54 us

profile of v5, /device:TPU:1, one launch (start us, length us, event | category | flops | bytes accessed | tf_op | source)
XLA Modules:
  0.0 35.5 jit_solution(15578317172783732399)
XLA Ops:
  0.6 33.3 %shard_map.50 = (bf16[8,192,256]{2,1,0:T(8,128)(2,1)S(1)}, bf16[28,96,128]{2,1,0:T(8,128)(2,1)S(1)}) custom-call(bf16[1,192,512]{2,1,0:T(8,128)(2,1)} %bitcast.5, bf16[8,192,256]{2,1,0:T(8,128)(2,1)} %bitcast.4, bf16[3,3,192,192]{3,2,1,0:T(8,128)(2,1)} %w_hbm.1), custom_call_target="tpu_custom_call" | custom-call | tf_op jit(solution)/shard_map/pallas_call | solution.py:410
  33.9 1.5 %shard_map.51 = (bf16[8,192,256]{2,1,0:T(8,128)(2,1)}, f32[9,192,192]{2,1,0:T(8,128)}) custom-call(bf16[8,192,256]{2,1,0:T(8,128)(2,1)S(1)} %get-tuple-element.6.ig_ref, bf16[28,96,128]{2,1,0:T(8,128)(2,1)S(1)} %get-tuple-element.7.sum_ref), custom_call_target="tpu_custom_call" | custom-call | tf_op jit(solution)/shard_map/pallas_call | solution.py:442

commit v6 on v5

--- a/solution.py
+++ b/solution.py
@@ -210,7 +210,7 @@
         pair_copy(j).wait_recv()
         outbox[j] = (part[base + j] + pair[j]).astype(BF16)
 
-        @pl.when(chip != owner_of(j))
+        @pl.when((chip != owner_of(j)) & (base + j < 27))
         def _():
             scatter_copy(j, 0).start()
 
@@ -218,7 +218,7 @@
         for i in range(count):
             j = far_first(i)
 
-            @pl.when(chip != owner_of(j))
+            @pl.when((chip != owner_of(j)) & (base + j < 27))
             def _():
                 scatter_copy(j, h).start()
 
@@ -244,7 +244,7 @@
         return (other * count + chips - 1) // chips
 
     def owns(other):
-        return (chunk_of(other) < count) & (owner_of(chunk_of(other)) == other)
+        return (base + chunk_of(other) < 27) & (chunk_of(other) < count) & (owner_of(chunk_of(other)) == other)
 
     mine = chunk_of(chip)
 
@@ -345,8 +345,10 @@
 
     for h in range(PIECES):
         for j in range(count):
-            forward_copy(j, h, 1 - core).wait_recv()
-            sum_ref[(1 - core) * count + j, cut(h)] = full[(1 - core) * count + j, cut(h)]
+            @pl.when((1 - core) * count + j < 27)
+            def _():
+                forward_copy(j, h, 1 - core).wait_recv()
+                sum_ref[(1 - core) * count + j, cut(h)] = full[(1 - core) * count + j, cut(h)]
 
     outgoing(lambda copy: copy.wait_send())
     for j in range(count):
@@ -354,9 +356,11 @@
 
     for h in range(PIECES):
         for j in range(count):
-            forward_copy(j, h, core).wait_send()
-
-            @pl.when(chip != owner_of(j))
+            @pl.when(base + j < 27)
+            def _():
+                forward_copy(j, h, core).wait_send()
+
+            @pl.when((chip != owner_of(j)) & (base + j < 27))
             def _():
                 scatter_copy(j, h).wait_send()
 

time: 35.6 us -> 35.1 us (0.986)
  Pallas kernels: 34.8 us -> 34.3 us
    pallas_call x1, Pallas kernels: 33.3 us -> 32.8 us  [per_device(): pl.pallas_call(functools.partial(step_kernel, n_rows, n_cols, scale), out...]
where the time goes in v6:
time: 35.1 us; the launch traced here: 34.9 us
  Pallas kernels  34.3 us (98%)
  between operations  0.64 us (2%)
    pallas_call x1, Pallas kernels, per_device(): pl.pallas_call(functools.partial(step_kernel, n_rows, n_cols, scale), out...  32.8 us
    pallas_call x1, Pallas kernels, per_device(): pl.pallas_call(unpack_kernel, out_shape=(jax.ShapeDtypeStruct(inputs.shap...  1.54 us

profile of v6, /device:TPU:1, one launch (start us, length us, event | category | flops | bytes accessed | tf_op | source)
XLA Modules:
  0.0 34.9 jit_solution(16252520301653024611)
XLA Ops:
  0.6 32.8 %shard_map.50 = (bf16[8,192,256]{2,1,0:T(8,128)(2,1)S(1)}, bf16[28,96,128]{2,1,0:T(8,128)(2,1)S(1)}) custom-call(bf16[1,192,512]{2,1,0:T(8,128)(2,1)} %bitcast.5, bf16[8,192,256]{2,1,0:T(8,128)(2,1)} %bitcast.4, bf16[3,3,192,192]{3,2,1,0:T(8,128)(2,1)} %w_hbm.1), custom_call_target="tpu_custom_call" | custom-call | tf_op jit(solution)/shard_map/pallas_call | solution.py:414
  33.4 1.5 %shard_map.51 = (bf16[8,192,256]{2,1,0:T(8,128)(2,1)}, f32[9,192,192]{2,1,0:T(8,128)}) custom-call(bf16[8,192,256]{2,1,0:T(8,128)(2,1)S(1)} %get-tuple-element.6.ig_ref, bf16[28,96,128]{2,1,0:T(8,128)(2,1)S(1)} %get-tuple-element.7.sum_ref), custom_call_target="tpu_custom_call" | custom-call | tf_op jit(solution)/shard_map/pallas_call | solution.py:446
